TPU v7x, 32 devices: a whole 2x2x4 slice. The times are simulated.
32 devices in a mesh: dp: 2 (over y), expert: 16 (over z, x, core).
Axes of the slice: x: 2, y: 2, z: 4, core: 2. Of those that a mesh axis runs over, the one named last changes fastest.
Arguments:
- tokens: bfloat16 [256, 2880], P(('dp', 'expert')), may hold values from -6 to 6
- routes: int32 [2, 256, 4], P(None, ('dp', 'expert')), may hold values from 0 to 15, all different within a row; in each aligned block of 8 rows (0 to 7, 8 to 15, ..., all dimensions but the last counted through in order) at most 4 rows name the same one
- placement: int32 [2, 16], replicated, may hold values from 0 to 15, each once within a row
- up_weight: bfloat16 [2, 16, 2880, 1440], P(None, 'expert', None, 'dp'), may hold values from -0.109375 to 0.109375
- down_weight: bfloat16 [2, 16, 1440, 2880], P(None, 'expert', 'dp'), may hold values from -0.15625 to 0.15625
- router_weight: bfloat16 [2, 16, 2880], P(None, 'expert'), may hold values from -0.21875 to 0.21875
Outputs:
- final_stream: bfloat16 [256, 2880], P(('dp', 'expert'))
Inputs may be any that keep to these rules, and one draw needn't show every extreme that they name: `routes`: each row names 4 different experts. Within one layer's rows of one device no expert is named by more than 4 rows, and some device names some expert exactly 4 times. `placement`: each layer's row is a permutation of the slots.
All inputs are finite; a program needn't handle non-finite values.
Results may differ from a plain program's by a relative error of at most 0.008.
Values may be sent and summed in bfloat16 or wider, within the bound.
A program may use at most 64 MiB of HBM per device.

v0:
```python
import jax
import jax.numpy as jnp
from jax import lax
from jax.sharding import PartitionSpec as P


def rms_rows(stream):
    values = stream.astype(jnp.float32)
    inverse = lax.rsqrt(jnp.mean(values * values, axis=-1, keepdims=True) + 1e-05)
    return (values * inverse).astype(jnp.bfloat16)


def slot_table(route_rows, place_row, columns, capacity):
    tok_rows, top_k = route_rows.shape
    experts = place_row.shape[0]
    matches = route_rows[:, :, None] == jnp.arange(experts, dtype=jnp.int32)[None, None, :]
    target = jnp.sum(jnp.where(matches, place_row[None, None, :], 0), axis=2).reshape(-1)
    row_count = target.shape[0]
    positions = jnp.arange(row_count, dtype=jnp.int32)
    earlier = (positions[None, :] < positions[:, None]) & (target[None, :] == target[:, None])
    row_rank = jnp.sum(earlier.astype(jnp.int32), axis=1)
    placed = (target[:, None, None] == jnp.arange(columns, dtype=jnp.int32)[None, :, None]) & (
        row_rank[:, None, None] == jnp.arange(capacity, dtype=jnp.int32)[None, None, :]
    )
    slot_map = jnp.sum(
        placed.reshape(tok_rows, top_k, columns, capacity).astype(jnp.float32), axis=1
    )
    return jnp.transpose(slot_map, (1, 2, 0))


def per_device(tokens, routes, placement, up_weight, down_weight, router_weight):
    groups = lax.axis_size("dp")
    columns = lax.axis_size("expert")
    tok_rows = tokens.shape[0]
    top_k = routes.shape[2]
    capacity = 2 * tok_rows * top_k // columns

    def layer_step(stream, packed):
        route_rows, place_row, up_part, down_part, router_part = packed
        normed = rms_rows(stream)
        slot_map = slot_table(route_rows, place_row, columns, capacity)
        outgoing = jnp.einsum(
            "jct,td->jcd", slot_map.astype(jnp.bfloat16), normed, preferred_element_type=jnp.float32
        ).astype(jnp.bfloat16)
        arrived = lax.all_to_all(
            outgoing, "expert", split_axis=0, concat_axis=0, tiled=True
        ).reshape(columns * capacity, -1)
        affinity = jax.nn.sigmoid(
            jnp.dot(arrived, router_part[0], preferred_element_type=jnp.float32)
        ).astype(jnp.bfloat16)
        all_rows, all_gates = (
            lax.all_gather(arrived, "dp", axis=0, tiled=True),
            lax.all_gather(affinity, "dp", axis=0, tiled=True),
        )
        hidden = jax.nn.silu(
            jnp.dot(all_rows, up_part[0], preferred_element_type=jnp.float32)
        ).astype(jnp.bfloat16)
        part_sums = jnp.dot(hidden, down_part[0], preferred_element_type=jnp.float32).astype(
            jnp.bfloat16
        )
        part_sums = part_sums.reshape(groups, columns, capacity, -1)
        all_gates = all_gates.reshape(groups, columns, capacity)
        returned, gates_back = (
            lax.all_to_all(
                lax.all_to_all(part_sums, "dp", split_axis=0, concat_axis=0, tiled=True),
                "expert",
                split_axis=1,
                concat_axis=1,
                tiled=True,
            ),
            lax.all_to_all(
                lax.all_to_all(all_gates, "dp", split_axis=0, concat_axis=0, tiled=True),
                "expert",
                split_axis=1,
                concat_axis=1,
                tiled=True,
            ),
        )
        weights = slot_map * gates_back[0].astype(jnp.float32)[:, :, None]
        numerator = jnp.einsum(
            "ect,gecd->td",
            weights.astype(jnp.bfloat16),
            returned,
            preferred_element_type=jnp.float32,
        )
        denominator = jnp.sum(weights, axis=(0, 1))
        updated = stream.astype(jnp.float32) + numerator / jnp.maximum(denominator, 0.5)[:, None]
        return (updated.astype(jnp.bfloat16), None)

    result_stream, unused = lax.scan(
        layer_step, tokens, (routes, placement, up_weight, down_weight, router_weight)
    )
    return result_stream


def solution(mesh):
    return jax.shard_map(
        per_device,
        mesh=mesh,
        in_specs=(
            P(("dp", "expert"), None),
            P(None, ("dp", "expert"), None),
            P(),
            P(None, "expert", None, "dp"),
            P(None, "expert", "dp", None),
            P(None, "expert", None),
        ),
        out_specs=P(("dp", "expert"), None),
        check_vma=False,
    )
```

profile of v0, /device:TPU:0, one launch (start us, length us, event | category | flops | bytes accessed | tf_op | source)
XLA Modules:
  0.0 197.5 jit_solution(17094374580464921686)
XLA Ops:
  0.0 0.8 copy.73
  0.8 196.1 %while.10 = (s32[]{:T(128)}, bf16[8,2880]{1,0:T(8,128)(2,1)S(1)}, s32[2,8,4]{1,2,0:T(4,128)}, s32[2,16]{1,0:T(2,128)}, bf16[2,1,2880]{2,0,1:T(2,128)(2,1)}, /*in...) while((s32[]{:T(128)}, bf16[8,2880]{1,0:T(8,128)(2,1)S(1)}, ...), condition=%wide.region_7.8_spmd, body=%wide.region_0.7_spmd.sunk | while | flops 1069763072 | bytes 25014808 | solution.py:90
  0.8 0.7 fusion.67
  1.5 0.7 dynamic-slice_bitcast_fusion.2
  2.2 0.2 select_reduce_fusion.2
  2.5 0.1 fusion.66
  2.8 0.2 convert_reduce_fusion.6
  3.2 0.3 convolution_convert_fusion.2
  3.6 0.9 copy.58
  4.4 7.4 %all-to-all-start = ((bf16[16,4,2880]{2,1,0:T(4,128)(2,1)}), bf16[16,4,2880]{2,1,0:T(4,128)(2,1)S(1)}, u32[]{:S(2)}, u32[]{:S(2)}) async-start(bf16[16,4,2880]{2,1,0:T(4,128)(2,1)} %copy.58), calls=%async_computation | async-start | bytes 753664 | tf_op jit(solution)/shard_map/while/body/eval_jaxpr/all_to_all | solution.py:45
  11.8 1.2 dynamic-slice.2
  13.7 10.0 %all-to-all-done = bf16[16,4,2880]{2,1,0:T(4,128)(2,1)S(1)} async-done(((bf16[16,4,2880]{2,1,0:T(4,128)(2,1)}), bf16[16,4,2880]{2,1,0:T(4,128)(2,1)S(1)}, u32[]{:S(2)}, u32[]{:S(2)}) %all-to-all-start) | async-done | bytes 368672 | tf_op jit(solution)/shard_map/while/body/eval_jaxpr/all_to_all | solution.py:45
  23.7 0.2 reshape.105
  23.9 11.4 %all_gather.7 = bf16[128,2880]{1,0:T(8,128)(2,1)S(1)} all-gather(bf16[64,2880]{1,0:T(8,128)(2,1)S(1)} %reshape.105), channel_id=1, replica_groups=mesh['dp'=2,'expert'=16] {'dp'}, dimensions={0}, use_global_device_ids=true | all-gather | bytes 1105920 | tf_op jit(solution)/shard_map/while/body/eval_jaxpr/all_gather | solution.py:52
  35.3 0.9 fusion.69
  36.2 0.3 dynamic-update-slice.2
  36.5 4.9 %all-reduce.2 = bf16[128]{0:T(256)(128)(2,1)S(1)} all-reduce(bf16[128]{0:T(256)(128)(2,1)S(1)} %dynamic-update-slice.2), channel_id=1, replica_groups=mesh['dp'=2,'expert'=16] {'dp'}, use_global_device_ids=true, to_apply=%add | all-reduce | flops 128 | bytes 512 | tf_op jit(solution)/shard_map/while
  41.4 0.1 reshape.107
  41.5 0.7 copy.61
  42.2 3.2 %all-to-all-start.3 = ((bf16[2,16,4]{1,2,0:T(4,128)(2,1)}), bf16[2,16,4]{1,2,0:T(4,128)(2,1)S(1)}, u32[]{:S(2)}, u32[]{:S(2)}) async-start(bf16[2,16,4]{1,2,0:T(4,128)(2,1)} %copy.61), calls=%async_computation.3 | async-start | bytes 4096 | tf_op jit(solution)/shard_map/while/body/eval_jaxpr/all_to_all | solution.py:72
  45.4 8.2 %fusion.68 = bf16[128,2880]{0,1:T(8,128)(2,1)S(1)} fusion(bf16[2,1,720,2880]{3,2,1,0:T(8,128)(2,1)} %get-tuple-element.130, s32[]{:T(128)} %get-tuple-element.112, bf16[128,2880]{1,0:T(8,128)(2,1)S(1)} %all_gather.7, bf16[2,1,2880,720]{2,3,1,0:T(8,128)(2,1)} %get-tuple-element.129), kind=kOutput, calls=%fused_computation.6.clone.1 | convolution fusion | flops 1062512640 | bytes 9954304 | tf_op jit(solution)/shard_map/while/body/eval_jaxpr/dot_general | solution.py:58
  53.6 0.4 copy.59
  54.0 1.1 reshape.106
  55.1 3.5 %all-to-all-start.1 = ((bf16[2,16,4,2880]{3,2,1,0:T(4,128)(2,1)}), bf16[2,16,4,2880]{3,2,1,0:T(4,128)(2,1)S(1)}, u32[]{:S(2)}, u32[]{:S(2)}) async-start(bf16[2,16,4,2880]{3,2,1,0:T(4,128)(2,1)} %reshape.106), calls=%async_computation.1 | async-start | bytes 1507328 | tf_op jit(solution)/shard_map/while/body/eval_jaxpr/all_to_all | solution.py:65
  58.6 0.7 copy.62
  59.3 8.3 %all-to-all-done.1 = bf16[2,16,4,2880]{3,2,1,0:T(4,128)(2,1)S(1)} async-done(((bf16[2,16,4,2880]{3,2,1,0:T(4,128)(2,1)}), bf16[2,16,4,2880]{3,2,1,0:T(4,128)(2,1)S(1)}, u32[]{:S(2)}, u32[]{:S(2)}) %all-to-all-start.1) | async-done | bytes 737312 | tf_op jit(solution)/shard_map/while/body/eval_jaxpr/all_to_all | solution.py:65
  67.6 3.9 %all-to-all-start.4 = ((bf16[2,16,4]{2,0,1:T(2,128)(2,1)}), bf16[2,16,4]{2,0,1:T(2,128)(2,1)S(1)}, u32[]{:S(2)}, u32[]{:S(2)}) async-start(bf16[2,16,4]{2,0,1:T(2,128)(2,1)} %copy.62), calls=%async_computation.4 | async-start | bytes 16384 | tf_op jit(solution)/shard_map/while/body/eval_jaxpr/all_to_all | solution.py:71
  71.5 1.1 copy.60
  72.6 5.2 %all-to-all-done.4 = bf16[2,16,4]{2,0,1:T(2,128)(2,1)S(1)} async-done(((bf16[2,16,4]{2,0,1:T(2,128)(2,1)}), bf16[2,16,4]{2,0,1:T(2,128)(2,1)S(1)}, u32[]{:S(2)}, u32[]{:S(2)}) %all-to-all-start.4) | async-done | bytes 288 | tf_op jit(solution)/shard_map/while/body/eval_jaxpr/all_to_all | solution.py:71
  77.8 3.6 %all-to-all-start.2 = ((bf16[2,16,4,2880]{3,2,0,1:T(4,128)(2,1)}), bf16[2,16,4,2880]{3,2,0,1:T(4,128)(2,1)S(1)}, u32[]{:S(2)}, u32[]{:S(2)}) async-start(bf16[2,16,4,2880]{3,2,0,1:T(4,128)(2,1)} %copy.60), calls=%async_computation.2 | async-start | bytes 1507328 | tf_op jit(solution)/shard_map/while/body/eval_jaxpr/all_to_all | solution.py:64
  81.6 0.1 multiply_reduce_fusion.2
  81.7 17.9 %all-to-all-done.2 = bf16[2,16,4,2880]{3,2,0,1:T(4,128)(2,1)S(1)} async-done(((bf16[2,16,4,2880]{3,2,0,1:T(4,128)(2,1)}), bf16[2,16,4,2880]{3,2,0,1:T(4,128)(2,1)S(1)}, u32[]{:S(2)}, u32[]{:S(2)}) %all-to-all-start.2) | async-done | bytes 737312 | tf_op jit(solution)/shard_map/while/body/eval_jaxpr/all_to_all | solution.py:64
  99.7 0.3 fusion.70
  100.0 0.7 fusion.67
  100.6 0.7 dynamic-slice_bitcast_fusion.2
  101.3 0.2 select_reduce_fusion.2
  101.7 0.1 fusion.66
  101.9 0.2 convert_reduce_fusion.6
  102.4 0.3 convolution_convert_fusion.2
  102.7 0.9 copy.58
  103.6 5.2 %all-to-all-start = ((bf16[16,4,2880]{2,1,0:T(4,128)(2,1)}), bf16[16,4,2880]{2,1,0:T(4,128)(2,1)S(1)}, u32[]{:S(2)}, u32[]{:S(2)}) async-start(bf16[16,4,2880]{2,1,0:T(4,128)(2,1)} %copy.58), calls=%async_computation | async-start | bytes 753664 | tf_op jit(solution)/shard_map/while/body/eval_jaxpr/all_to_all | solution.py:45
  108.8 1.2 dynamic-slice.2
  110.7 10.0 %all-to-all-done = bf16[16,4,2880]{2,1,0:T(4,128)(2,1)S(1)} async-done(((bf16[16,4,2880]{2,1,0:T(4,128)(2,1)}), bf16[16,4,2880]{2,1,0:T(4,128)(2,1)S(1)}, u32[]{:S(2)}, u32[]{:S(2)}) %all-to-all-start) | async-done | bytes 368672 | tf_op jit(solution)/shard_map/while/body/eval_jaxpr/all_to_all | solution.py:45
  120.6 0.2 reshape.105
  120.8 11.4 %all_gather.7 = bf16[128,2880]{1,0:T(8,128)(2,1)S(1)} all-gather(bf16[64,2880]{1,0:T(8,128)(2,1)S(1)} %reshape.105), channel_id=1, replica_groups=mesh['dp'=2,'expert'=16] {'dp'}, dimensions={0}, use_global_device_ids=true | all-gather | bytes 1105920 | tf_op jit(solution)/shard_map/while/body/eval_jaxpr/all_gather | solution.py:52
  132.3 0.9 fusion.69
  133.2 0.3 dynamic-update-slice.2
  133.4 4.9 %all-reduce.2 = bf16[128]{0:T(256)(128)(2,1)S(1)} all-reduce(bf16[128]{0:T(256)(128)(2,1)S(1)} %dynamic-update-slice.2), channel_id=1, replica_groups=mesh['dp'=2,'expert'=16] {'dp'}, use_global_device_ids=true, to_apply=%add | all-reduce | flops 128 | bytes 512 | tf_op jit(solution)/shard_map/while
  138.4 0.7 copy.61
  139.1 3.2 %all-to-all-start.3 = ((bf16[2,16,4]{1,2,0:T(4,128)(2,1)}), bf16[2,16,4]{1,2,0:T(4,128)(2,1)S(1)}, u32[]{:S(2)}, u32[]{:S(2)}) async-start(bf16[2,16,4]{1,2,0:T(4,128)(2,1)} %copy.61), calls=%async_computation.3 | async-start | bytes 4096 | tf_op jit(solution)/shard_map/while/body/eval_jaxpr/all_to_all | solution.py:72
  142.3 8.2 %fusion.68 = bf16[128,2880]{0,1:T(8,128)(2,1)S(1)} fusion(bf16[2,1,720,2880]{3,2,1,0:T(8,128)(2,1)} %get-tuple-element.130, s32[]{:T(128)} %get-tuple-element.112, bf16[128,2880]{1,0:T(8,128)(2,1)S(1)} %all_gather.7, bf16[2,1,2880,720]{2,3,1,0:T(8,128)(2,1)} %get-tuple-element.129), kind=kOutput, calls=%fused_computation.6.clone.1 | convolution fusion | flops 1062512640 | bytes 9954304 | tf_op jit(solution)/shard_map/while/body/eval_jaxpr/dot_general | solution.py:58
  150.6 0.4 copy.59
  150.9 1.1 reshape.106
  152.0 3.5 %all-to-all-start.1 = ((bf16[2,16,4,2880]{3,2,1,0:T(4,128)(2,1)}), bf16[2,16,4,2880]{3,2,1,0:T(4,128)(2,1)S(1)}, u32[]{:S(2)}, u32[]{:S(2)}) async-start(bf16[2,16,4,2880]{3,2,1,0:T(4,128)(2,1)} %reshape.106), calls=%async_computation.1 | async-start | bytes 1507328 | tf_op jit(solution)/shard_map/while/body/eval_jaxpr/all_to_all | solution.py:65
  155.5 0.7 copy.62
  156.2 8.3 %all-to-all-done.1 = bf16[2,16,4,2880]{3,2,1,0:T(4,128)(2,1)S(1)} async-done(((bf16[2,16,4,2880]{3,2,1,0:T(4,128)(2,1)}), bf16[2,16,4,2880]{3,2,1,0:T(4,128)(2,1)S(1)}, u32[]{:S(2)}, u32[]{:S(2)}) %all-to-all-start.1) | async-done | bytes 737312 | tf_op jit(solution)/shard_map/while/body/eval_jaxpr/all_to_all | solution.py:65
  164.5 3.9 %all-to-all-start.4 = ((bf16[2,16,4]{2,0,1:T(2,128)(2,1)}), bf16[2,16,4]{2,0,1:T(2,128)(2,1)S(1)}, u32[]{:S(2)}, u32[]{:S(2)}) async-start(bf16[2,16,4]{2,0,1:T(2,128)(2,1)} %copy.62), calls=%async_computation.4 | async-start | bytes 16384 | tf_op jit(solution)/shard_map/while/body/eval_jaxpr/all_to_all | solution.py:71
  168.4 1.1 copy.60
  169.6 5.2 %all-to-all-done.4 = bf16[2,16,4]{2,0,1:T(2,128)(2,1)S(1)} async-done(((bf16[2,16,4]{2,0,1:T(2,128)(2,1)}), bf16[2,16,4]{2,0,1:T(2,128)(2,1)S(1)}, u32[]{:S(2)}, u32[]{:S(2)}) %all-to-all-start.4) | async-done | bytes 288 | tf_op jit(solution)/shard_map/while/body/eval_jaxpr/all_to_all | solution.py:71
  174.8 3.6 %all-to-all-start.2 = ((bf16[2,16,4,2880]{3,2,0,1:T(4,128)(2,1)}), bf16[2,16,4,2880]{3,2,0,1:T(4,128)(2,1)S(1)}, u32[]{:S(2)}, u32[]{:S(2)}) async-start(bf16[2,16,4,2880]{3,2,0,1:T(4,128)(2,1)} %copy.60), calls=%async_computation.2 | async-start | bytes 1507328 | tf_op jit(solution)/shard_map/while/body/eval_jaxpr/all_to_all | solution.py:64
  178.5 0.1 multiply_reduce_fusion.2
  178.6 17.9 %all-to-all-done.2 = bf16[2,16,4,2880]{3,2,0,1:T(4,128)(2,1)S(1)} async-done(((bf16[2,16,4,2880]{3,2,0,1:T(4,128)(2,1)}), bf16[2,16,4,2880]{3,2,0,1:T(4,128)(2,1)S(1)}, u32[]{:S(2)}, u32[]{:S(2)}) %all-to-all-start.2) | async-done | bytes 737312 | tf_op jit(solution)/shard_map/while/body/eval_jaxpr/all_to_all | solution.py:64
  196.6 0.3 fusion.70
  196.9 0.6 copy-done
  (30 shorter events, 1.5 us)
Async XLA Ops:
  4.4 19.3 %all-to-all-start = ((bf16[16,4,2880]{2,1,0:T(4,128)(2,1)}), bf16[16,4,2880]{2,1,0:T(4,128)(2,1)S(1)}, u32[]{:S(2)}, u32[]{:S(2)}) async-start(bf16[16,4,2880]{2,1,0:T(4,128)(2,1)} %copy.58), calls=%async_computation | async-start | bytes 753664 | tf_op jit(solution)/shard_map/while/body/eval_jaxpr/all_to_all | solution.py:45
  42.2 12.9 %all-to-all-start.3 = ((bf16[2,16,4]{1,2,0:T(4,128)(2,1)}), bf16[2,16,4]{1,2,0:T(4,128)(2,1)S(1)}, u32[]{:S(2)}, u32[]{:S(2)}) async-start(bf16[2,16,4]{1,2,0:T(4,128)(2,1)} %copy.61), calls=%async_computation.3 | async-start | bytes 4096 | tf_op jit(solution)/shard_map/while/body/eval_jaxpr/all_to_all | solution.py:72
  55.1 12.5 %all-to-all-start.1 = ((bf16[2,16,4,2880]{3,2,1,0:T(4,128)(2,1)}), bf16[2,16,4,2880]{3,2,1,0:T(4,128)(2,1)S(1)}, u32[]{:S(2)}, u32[]{:S(2)}) async-start(bf16[2,16,4,2880]{3,2,1,0:T(4,128)(2,1)} %reshape.106), calls=%async_computation.1 | async-start | bytes 1507328 | tf_op jit(solution)/shard_map/while/body/eval_jaxpr/all_to_all | solution.py:65
  67.6 10.3 %all-to-all-start.4 = ((bf16[2,16,4]{2,0,1:T(2,128)(2,1)}), bf16[2,16,4]{2,0,1:T(2,128)(2,1)S(1)}, u32[]{:S(2)}, u32[]{:S(2)}) async-start(bf16[2,16,4]{2,0,1:T(2,128)(2,1)} %copy.62), calls=%async_computation.4 | async-start | bytes 16384 | tf_op jit(solution)/shard_map/while/body/eval_jaxpr/all_to_all | solution.py:71
  77.8 21.7 %all-to-all-start.2 = ((bf16[2,16,4,2880]{3,2,0,1:T(4,128)(2,1)}), bf16[2,16,4,2880]{3,2,0,1:T(4,128)(2,1)S(1)}, u32[]{:S(2)}, u32[]{:S(2)}) async-start(bf16[2,16,4,2880]{3,2,0,1:T(4,128)(2,1)} %copy.60), calls=%async_computation.2 | async-start | bytes 1507328 | tf_op jit(solution)/shard_map/while/body/eval_jaxpr/all_to_all | solution.py:64
  103.6 17.0 %all-to-all-start = ((bf16[16,4,2880]{2,1,0:T(4,128)(2,1)}), bf16[16,4,2880]{2,1,0:T(4,128)(2,1)S(1)}, u32[]{:S(2)}, u32[]{:S(2)}) async-start(bf16[16,4,2880]{2,1,0:T(4,128)(2,1)} %copy.58), calls=%async_computation | async-start | bytes 753664 | tf_op jit(solution)/shard_map/while/body/eval_jaxpr/all_to_all | solution.py:45
  139.1 12.9 %all-to-all-start.3 = ((bf16[2,16,4]{1,2,0:T(4,128)(2,1)}), bf16[2,16,4]{1,2,0:T(4,128)(2,1)S(1)}, u32[]{:S(2)}, u32[]{:S(2)}) async-start(bf16[2,16,4]{1,2,0:T(4,128)(2,1)} %copy.61), calls=%async_computation.3 | async-start | bytes 4096 | tf_op jit(solution)/shard_map/while/body/eval_jaxpr/all_to_all | solution.py:72
  152.0 12.5 %all-to-all-start.1 = ((bf16[2,16,4,2880]{3,2,1,0:T(4,128)(2,1)}), bf16[2,16,4,2880]{3,2,1,0:T(4,128)(2,1)S(1)}, u32[]{:S(2)}, u32[]{:S(2)}) async-start(bf16[2,16,4,2880]{3,2,1,0:T(4,128)(2,1)} %reshape.106), calls=%async_computation.1 | async-start | bytes 1507328 | tf_op jit(solution)/shard_map/while/body/eval_jaxpr/all_to_all | solution.py:65
  164.5 10.3 %all-to-all-start.4 = ((bf16[2,16,4]{2,0,1:T(2,128)(2,1)}), bf16[2,16,4]{2,0,1:T(2,128)(2,1)S(1)}, u32[]{:S(2)}, u32[]{:S(2)}) async-start(bf16[2,16,4]{2,0,1:T(2,128)(2,1)} %copy.62), calls=%async_computation.4 | async-start | bytes 16384 | tf_op jit(solution)/shard_map/while/body/eval_jaxpr/all_to_all | solution.py:71
  174.8 21.7 %all-to-all-start.2 = ((bf16[2,16,4,2880]{3,2,0,1:T(4,128)(2,1)}), bf16[2,16,4,2880]{3,2,0,1:T(4,128)(2,1)S(1)}, u32[]{:S(2)}, u32[]{:S(2)}) async-start(bf16[2,16,4,2880]{3,2,0,1:T(4,128)(2,1)} %copy.60), calls=%async_computation.2 | async-start | bytes 1507328 | tf_op jit(solution)/shard_map/while/body/eval_jaxpr/all_to_all | solution.py:64
  196.9 0.6 copy-start
where the time goes:
time: 199 us; the launch traced here: 198 us
  waiting for transfers between devices  82.7 us (42%)
  starting transfers between devices  41.1 us (21%)
  blocking collectives  32.7 us (16%)
  matrix products  19.4 us (10%)
  local copies, waits for them, and re-layouts  18.1 us (9%)
    all_to_all x2, waiting for transfers between devices, layer_step(): lax.all_to_all(lax.all_to_all(part_sums, 'dp', split_axis=0, concat_axis=...  35.8 us
    all_gather x2, blocking collectives, layer_step(): lax.all_gather(arrived, 'dp', axis=0, tiled=True)  22.9 us
    all_to_all x2, waiting for transfers between devices, layer_step(): lax.all_to_all(outgoing, 'expert', split_axis=0, concat_axis=0, tiled=True)  19.9 us
    all_to_all x2, waiting for transfers between devices, layer_step(): lax.all_to_all(part_sums, 'dp', split_axis=0, concat_axis=0, tiled=True)  16.5 us
    dot_general x2, matrix products, layer_step(): jnp.dot(hidden, down_part[0], preferred_element_type=jnp.float32)  16.4 us
    all_to_all x2, starting transfers between devices, layer_step(): lax.all_to_all(outgoing, 'expert', split_axis=0, concat_axis=0, tiled=True)  12.5 us
    all_to_all x2, waiting for transfers between devices, layer_step(): lax.all_to_all(lax.all_to_all(all_gates, 'dp', split_axis=0, concat_axis=...  10.5 us
    while x2, blocking collectives  9.82 us
  transfers between devices with their start and end apart: 10, of which 8 were waited for; matrix products, arithmetic and copies ran while one was open for 13% of the time, Pallas kernels for 0%

commit v1 on v0

--- a/solution.py
+++ b/solution.py
@@ -60,13 +60,21 @@
         )
         part_sums = part_sums.reshape(groups, columns, capacity, -1)
         all_gates = all_gates.reshape(groups, columns, capacity)
+
+        def _state_shifts_all(shard_in):
+            return jnp.concatenate(
+                jax.lax.all_to_all(
+                    jnp.stack(jnp.split(shard_in, jax.lax.axis_size("expert"), axis=1), axis=0),
+                    split_axis=0,
+                    axis_name="expert",
+                    concat_axis=0,
+                ),
+                axis=1,
+            )
+
         returned, gates_back = (
-            lax.all_to_all(
-                lax.all_to_all(part_sums, "dp", split_axis=0, concat_axis=0, tiled=True),
-                "expert",
-                split_axis=1,
-                concat_axis=1,
-                tiled=True,
+            _state_shifts_all(
+                lax.all_to_all(part_sums, "dp", split_axis=0, concat_axis=0, tiled=True)
             ),
             lax.all_to_all(
                 lax.all_to_all(all_gates, "dp", split_axis=0, concat_axis=0, tiled=True),

time: 199 us -> 212 us (1.065)
  local copies, waits for them, and re-layouts: 18.1 us -> 36.1 us
  waiting for transfers between devices: 82.7 us -> 72.3 us
  starting transfers between devices: 41.1 us -> 45.9 us
    while x8 -> x38, local copies, waits for them, and re-layouts: 3.18 us -> 22.1 us
    all_to_all x2, waiting for transfers between devices: 10.5 us -> 0.01 us  [layer_step(): lax.all_to_all(lax.all_to_all(all_gates, 'dp', split_axis=0, concat_axis=...]
    all_to_all x2, starting transfers between devices: 7.22 us -> 12 us  [_state_shifts_all(): jax.lax.all_to_all(jnp.stack(jnp.split(shard_in, jax.lax.axis_size('exper...]
    all_to_all x2 -> x0, local copies, waits for them, and re-layouts: 2.26 us -> none  [layer_step(): lax.all_to_all(part_sums, 'dp', split_axis=0, concat_axis=0, tiled=True)]
  transfers between devices with their start and end apart: 10 -> 10, of which waited for: 8 -> 6; matrix products, arithmetic and copies ran while one was open for 13% -> 21% of each run, Pallas kernels for 0% -> 0%
where the time goes in v1:
time: 212 us; the launch traced here: 211 us
  waiting for transfers between devices  72.3 us (34%)
  starting transfers between devices  45.9 us (22%)
  local copies, waits for them, and re-layouts  36.1 us (17%)
  blocking collectives  32.7 us (15%)
  matrix products  19.4 us (9%)
  other arithmetic  2.67 us (1%)
    all_to_all x2, waiting for transfers between devices, _state_shifts_all(): jax.lax.all_to_all(jnp.stack(jnp.split(shard_in, jax.lax.axis_size('exper...  35.8 us
    all_gather x2, blocking collectives, layer_step(): lax.all_gather(arrived, 'dp', axis=0, tiled=True)  22.9 us
    while x38, local copies, waits for them, and re-layouts  22.1 us
    all_to_all x2, waiting for transfers between devices, layer_step(): lax.all_to_all(outgoing, 'expert', split_axis=0, concat_axis=0, tiled=True)  19.9 us
    all_to_all x2, waiting for transfers between devices, layer_step(): lax.all_to_all(part_sums, 'dp', split_axis=0, concat_axis=0, tiled=True)  16.5 us
    dot_general x2, matrix products, layer_step(): jnp.dot(hidden, down_part[0], preferred_element_type=jnp.float32)  16.4 us
    all_to_all x2, starting transfers between devices, layer_step(): lax.all_to_all(outgoing, 'expert', split_axis=0, concat_axis=0, tiled=True)  12.6 us
    all_to_all x2, starting transfers between devices, _state_shifts_all(): jax.lax.all_to_all(jnp.stack(jnp.split(shard_in, jax.lax.axis_size('exper...  12 us
  transfers between devices with their start and end apart: 10, of which 6 were waited for; matrix products, arithmetic and copies ran while one was open for 21% of the time, Pallas kernels for 0%

profile of v1, /device:TPU:0, one launch (start us, length us, event | category | flops | bytes accessed | tf_op | source)
XLA Modules:
  0.0 210.7 jit_solution(16851115231067142079)
XLA Ops:
  0.0 0.8 copy.164
  0.8 209.3 %while.10 = (s32[]{:T(128)}, bf16[8,2880]{1,0:T(8,128)(2,1)S(1)}, s32[2,8,4]{1,2,0:T(4,128)}, s32[2,16]{1,0:T(2,128)}, bf16[2,1,2880]{2,0,1:T(2,128)(2,1)}, /*in...) while((s32[]{:T(128)}, bf16[8,2880]{1,0:T(8,128)(2,1)S(1)}, ...), condition=%wide.region_7.8_spmd, body=%wide.region_0.7_spmd.sunk | while | flops 1069763072 | bytes 25031192 | solution.py:98
  0.8 0.7 fusion.99
  1.5 0.7 dynamic-slice_bitcast_fusion.2
  3.6 0.9 copy.135
  4.4 7.4 %all-to-all-start = ((bf16[16,4,2880]{2,1,0:T(4,128)(2,1)}), bf16[16,4,2880]{2,1,0:T(4,128)(2,1)S(1)}, u32[]{:S(2)}, u32[]{:S(2)}) async-start(bf16[16,4,2880]{2,1,0:T(4,128)(2,1)} %copy.135), calls=%async_computation | async-start | bytes 753664 | tf_op jit(solution)/shard_map/while/body/eval_jaxpr/all_to_all | solution.py:45
  11.8 1.2 dynamic-slice.2
  13.7 10.0 %all-to-all-done = bf16[16,4,2880]{2,1,0:T(4,128)(2,1)S(1)} async-done(((bf16[16,4,2880]{2,1,0:T(4,128)(2,1)}), bf16[16,4,2880]{2,1,0:T(4,128)(2,1)S(1)}, u32[]{:S(2)}, u32[]{:S(2)}) %all-to-all-start) | async-done | bytes 368672 | tf_op jit(solution)/shard_map/while/body/eval_jaxpr/all_to_all | solution.py:45
  23.9 11.4 %all_gather.7 = bf16[128,2880]{1,0:T(8,128)(2,1)S(1)} all-gather(bf16[64,2880]{1,0:T(8,128)(2,1)S(1)} %reshape.108), channel_id=1, replica_groups=mesh['dp'=2,'expert'=16] {'dp'}, dimensions={0}, use_global_device_ids=true | all-gather | bytes 1105920 | tf_op jit(solution)/shard_map/while/body/eval_jaxpr/all_gather | solution.py:52
  35.3 0.9 fusion.117
  36.5 4.9 %all-reduce.2 = bf16[128]{0:T(256)(128)(2,1)S(1)} all-reduce(bf16[128]{0:T(256)(128)(2,1)S(1)} %dynamic-update-slice.66), channel_id=1, replica_groups=mesh['dp'=2,'expert'=16] {'dp'}, use_global_device_ids=true, to_apply=%add | all-reduce | flops 128 | bytes 512 | tf_op jit(solution)/shard_map/while
  41.5 0.7 copy.137
  42.2 3.2 %all-to-all-start.3 = ((bf16[2,16,4]{1,2,0:T(4,128)(2,1)}), bf16[2,16,4]{1,2,0:T(4,128)(2,1)S(1)}, u32[]{:S(2)}, u32[]{:S(2)}) async-start(bf16[2,16,4]{1,2,0:T(4,128)(2,1)} %copy.137), calls=%async_computation.3 | async-start | bytes 4096 | tf_op jit(solution)/shard_map/while/body/eval_jaxpr/all_to_all | solution.py:80
  45.4 8.2 %fusion.100 = bf16[128,2880]{0,1:T(8,128)(2,1)S(1)} fusion(bf16[2,1,720,2880]{3,2,1,0:T(8,128)(2,1)} %get-tuple-element.130, s32[]{:T(128)} %get-tuple-element.112, bf16[128,2880]{1,0:T(8,128)(2,1)S(1)} %all_gather.7, bf16[2,1,2880,720]{2,3,1,0:T(8,128)(2,1)} %get-tuple-element.129), kind=kOutput, calls=%fused_computation.6.clone.1 | convolution fusion | flops 1062512640 | bytes 9954304 | tf_op jit(solution)/shard_map/while/body/eval_jaxpr/dot_general | solution.py:58
  54.0 1.1 reshape.109
  55.1 3.5 %all-to-all-start.1 = ((bf16[2,16,4,2880]{3,2,1,0:T(4,128)(2,1)}), bf16[2,16,4,2880]{3,2,1,0:T(4,128)(2,1)S(1)}, u32[]{:S(2)}, u32[]{:S(2)}) async-start(bf16[2,16,4,2880]{3,2,1,0:T(4,128)(2,1)} %reshape.109), calls=%async_computation.1 | async-start | bytes 1507328 | tf_op jit(solution)/shard_map/while/body/eval_jaxpr/all_to_all | solution.py:77
  58.6 0.7 copy.138
  59.3 8.3 %all-to-all-done.1 = bf16[2,16,4,2880]{3,2,1,0:T(4,128)(2,1)S(1)} async-done(((bf16[2,16,4,2880]{3,2,1,0:T(4,128)(2,1)}), bf16[2,16,4,2880]{3,2,1,0:T(4,128)(2,1)S(1)}, u32[]{:S(2)}, u32[]{:S(2)}) %all-to-all-start.1) | async-done | bytes 737312 | tf_op jit(solution)/shard_map/while/body/eval_jaxpr/all_to_all | solution.py:77
  67.6 3.9 %all-to-all-start.4 = ((bf16[2,16,4]{2,0,1:T(2,128)(2,1)}), bf16[2,16,4]{2,0,1:T(2,128)(2,1)S(1)}, u32[]{:S(2)}, u32[]{:S(2)}) async-start(bf16[2,16,4]{2,0,1:T(2,128)(2,1)} %copy.138), calls=%async_computation.4 | async-start | bytes 16384 | tf_op jit(solution)/shard_map/while/body/eval_jaxpr/all_to_all | solution.py:79
  71.5 0.6 fusion.101
  72.1 0.6 fusion.102
  72.8 0.6 fusion.103
  74.0 0.6 fusion.105
  74.7 0.6 fusion.106
  75.3 0.6 fusion.107
  75.9 0.6 fusion.108
  77.2 0.6 fusion.110
  78.4 0.6 fusion.112
  79.1 0.6 fusion.113
  79.7 0.6 fusion.114
  81.0 0.6 fusion.116
  81.6 6.0 %all-to-all-start.2 = ((bf16[16,2,1,4,2880]{4,3,1,2,0:T(4,128)(2,1)}), bf16[16,2,1,4,2880]{4,3,1,2,0:T(4,128)(2,1)S(1)}, u32[]{:S(2)}, u32[]{:S(2)}) async-start(bf16[16,2,1,4,2880]{4,3,1,2,0:T(4,128)(2,1)} %fusion.116), calls=%async_computation.2 | async-start | bytes 1507328 | tf_op jit(solution)/shard_map/while/body/eval_jaxpr/all_to_all | solution.py:66
  87.9 17.9 %all-to-all-done.2 = bf16[16,2,1,4,2880]{4,3,1,2,0:T(4,128)(2,1)S(1)} async-done(((bf16[16,2,1,4,2880]{4,3,1,2,0:T(4,128)(2,1)}), bf16[16,2,1,4,2880]{4,3,1,2,0:T(4,128)(2,1)S(1)}, u32[]{:S(2)}, u32[]{:S(2)}) %all-to-all-start.2) | async-done | bytes 737312 | tf_op jit(solution)/shard_map/while/body/eval_jaxpr/all_to_all | solution.py:66
  106.5 0.7 fusion.99
  107.2 0.7 dynamic-slice_bitcast_fusion.2
  109.3 0.9 copy.135
  110.2 5.2 %all-to-all-start = ((bf16[16,4,2880]{2,1,0:T(4,128)(2,1)}), bf16[16,4,2880]{2,1,0:T(4,128)(2,1)S(1)}, u32[]{:S(2)}, u32[]{:S(2)}) async-start(bf16[16,4,2880]{2,1,0:T(4,128)(2,1)} %copy.135), calls=%async_computation | async-start | bytes 753664 | tf_op jit(solution)/shard_map/while/body/eval_jaxpr/all_to_all | solution.py:45
  115.4 1.2 dynamic-slice.2
  117.3 10.0 %all-to-all-done = bf16[16,4,2880]{2,1,0:T(4,128)(2,1)S(1)} async-done(((bf16[16,4,2880]{2,1,0:T(4,128)(2,1)}), bf16[16,4,2880]{2,1,0:T(4,128)(2,1)S(1)}, u32[]{:S(2)}, u32[]{:S(2)}) %all-to-all-start) | async-done | bytes 368672 | tf_op jit(solution)/shard_map/while/body/eval_jaxpr/all_to_all | solution.py:45
  127.4 11.4 %all_gather.7 = bf16[128,2880]{1,0:T(8,128)(2,1)S(1)} all-gather(bf16[64,2880]{1,0:T(8,128)(2,1)S(1)} %reshape.108), channel_id=1, replica_groups=mesh['dp'=2,'expert'=16] {'dp'}, dimensions={0}, use_global_device_ids=true | all-gather | bytes 1105920 | tf_op jit(solution)/shard_map/while/body/eval_jaxpr/all_gather | solution.py:52
  138.9 0.9 fusion.117
  140.0 4.9 %all-reduce.2 = bf16[128]{0:T(256)(128)(2,1)S(1)} all-reduce(bf16[128]{0:T(256)(128)(2,1)S(1)} %dynamic-update-slice.66), channel_id=1, replica_groups=mesh['dp'=2,'expert'=16] {'dp'}, use_global_device_ids=true, to_apply=%add | all-reduce | flops 128 | bytes 512 | tf_op jit(solution)/shard_map/while
  145.1 0.7 copy.137
  145.8 3.2 %all-to-all-start.3 = ((bf16[2,16,4]{1,2,0:T(4,128)(2,1)}), bf16[2,16,4]{1,2,0:T(4,128)(2,1)S(1)}, u32[]{:S(2)}, u32[]{:S(2)}) async-start(bf16[2,16,4]{1,2,0:T(4,128)(2,1)} %copy.137), calls=%async_computation.3 | async-start | bytes 4096 | tf_op jit(solution)/shard_map/while/body/eval_jaxpr/all_to_all | solution.py:80
  149.0 8.2 %fusion.100 = bf16[128,2880]{0,1:T(8,128)(2,1)S(1)} fusion(bf16[2,1,720,2880]{3,2,1,0:T(8,128)(2,1)} %get-tuple-element.130, s32[]{:T(128)} %get-tuple-element.112, bf16[128,2880]{1,0:T(8,128)(2,1)S(1)} %all_gather.7, bf16[2,1,2880,720]{2,3,1,0:T(8,128)(2,1)} %get-tuple-element.129), kind=kOutput, calls=%fused_computation.6.clone.1 | convolution fusion | flops 1062512640 | bytes 9954304 | tf_op jit(solution)/shard_map/while/body/eval_jaxpr/dot_general | solution.py:58
  157.6 1.1 reshape.109
  158.6 3.5 %all-to-all-start.1 = ((bf16[2,16,4,2880]{3,2,1,0:T(4,128)(2,1)}), bf16[2,16,4,2880]{3,2,1,0:T(4,128)(2,1)S(1)}, u32[]{:S(2)}, u32[]{:S(2)}) async-start(bf16[2,16,4,2880]{3,2,1,0:T(4,128)(2,1)} %reshape.109), calls=%async_computation.1 | async-start | bytes 1507328 | tf_op jit(solution)/shard_map/while/body/eval_jaxpr/all_to_all | solution.py:77
  162.2 0.7 copy.138
  162.9 8.3 %all-to-all-done.1 = bf16[2,16,4,2880]{3,2,1,0:T(4,128)(2,1)S(1)} async-done(((bf16[2,16,4,2880]{3,2,1,0:T(4,128)(2,1)}), bf16[2,16,4,2880]{3,2,1,0:T(4,128)(2,1)S(1)}, u32[]{:S(2)}, u32[]{:S(2)}) %all-to-all-start.1) | async-done | bytes 737312 | tf_op jit(solution)/shard_map/while/body/eval_jaxpr/all_to_all | solution.py:77
  171.1 3.9 %all-to-all-start.4 = ((bf16[2,16,4]{2,0,1:T(2,128)(2,1)}), bf16[2,16,4]{2,0,1:T(2,128)(2,1)S(1)}, u32[]{:S(2)}, u32[]{:S(2)}) async-start(bf16[2,16,4]{2,0,1:T(2,128)(2,1)} %copy.138), calls=%async_computation.4 | async-start | bytes 16384 | tf_op jit(solution)/shard_map/while/body/eval_jaxpr/all_to_all | solution.py:79
  175.1 0.6 fusion.101
  175.7 0.6 fusion.102
  176.3 0.6 fusion.103
  177.6 0.6 fusion.105
  178.2 0.6 fusion.106
  178.9 0.6 fusion.107
  179.5 0.6 fusion.108
  180.7 0.6 fusion.110
  182.0 0.6 fusion.112
  182.6 0.6 fusion.113
  183.3 0.6 fusion.114
  184.5 0.6 fusion.116
  185.2 6.0 %all-to-all-start.2 = ((bf16[16,2,1,4,2880]{4,3,1,2,0:T(4,128)(2,1)}), bf16[16,2,1,4,2880]{4,3,1,2,0:T(4,128)(2,1)S(1)}, u32[]{:S(2)}, u32[]{:S(2)}) async-start(bf16[16,2,1,4,2880]{4,3,1,2,0:T(4,128)(2,1)} %fusion.116), calls=%async_computation.2 | async-start | bytes 1507328 | tf_op jit(solution)/shard_map/while/body/eval_jaxpr/all_to_all | solution.py:66
  191.4 17.9 %all-to-all-done.2 = bf16[16,2,1,4,2880]{4,3,1,2,0:T(4,128)(2,1)S(1)} async-done(((bf16[16,2,1,4,2880]{4,3,1,2,0:T(4,128)(2,1)}), bf16[16,2,1,4,2880]{4,3,1,2,0:T(4,128)(2,1)S(1)}, u32[]{:S(2)}, u32[]{:S(2)}) %all-to-all-start.2) | async-done | bytes 737312 | tf_op jit(solution)/shard_map/while/body/eval_jaxpr/all_to_all | solution.py:66
  (60 shorter events, 12.1 us)
Async XLA Ops:
  4.4 19.3 %all-to-all-start = ((bf16[16,4,2880]{2,1,0:T(4,128)(2,1)}), bf16[16,4,2880]{2,1,0:T(4,128)(2,1)S(1)}, u32[]{:S(2)}, u32[]{:S(2)}) async-start(bf16[16,4,2880]{2,1,0:T(4,128)(2,1)} %copy.135), calls=%async_computation | async-start | bytes 753664 | tf_op jit(solution)/shard_map/while/body/eval_jaxpr/all_to_all | solution.py:45
  42.2 12.9 %all-to-all-start.3 = ((bf16[2,16,4]{1,2,0:T(4,128)(2,1)}), bf16[2,16,4]{1,2,0:T(4,128)(2,1)S(1)}, u32[]{:S(2)}, u32[]{:S(2)}) async-start(bf16[2,16,4]{1,2,0:T(4,128)(2,1)} %copy.137), calls=%async_computation.3 | async-start | bytes 4096 | tf_op jit(solution)/shard_map/while/body/eval_jaxpr/all_to_all | solution.py:80
  55.1 12.5 %all-to-all-start.1 = ((bf16[2,16,4,2880]{3,2,1,0:T(4,128)(2,1)}), bf16[2,16,4,2880]{3,2,1,0:T(4,128)(2,1)S(1)}, u32[]{:S(2)}, u32[]{:S(2)}) async-start(bf16[2,16,4,2880]{3,2,1,0:T(4,128)(2,1)} %reshape.109), calls=%async_computation.1 | async-start | bytes 1507328 | tf_op jit(solution)/shard_map/while/body/eval_jaxpr/all_to_all | solution.py:77
  67.6 14.1 %all-to-all-start.4 = ((bf16[2,16,4]{2,0,1:T(2,128)(2,1)}), bf16[2,16,4]{2,0,1:T(2,128)(2,1)S(1)}, u32[]{:S(2)}, u32[]{:S(2)}) async-start(bf16[2,16,4]{2,0,1:T(2,128)(2,1)} %copy.138), calls=%async_computation.4 | async-start | bytes 16384 | tf_op jit(solution)/shard_map/while/body/eval_jaxpr/all_to_all | solution.py:79
  81.6 24.2 %all-to-all-start.2 = ((bf16[16,2,1,4,2880]{4,3,1,2,0:T(4,128)(2,1)}), bf16[16,2,1,4,2880]{4,3,1,2,0:T(4,128)(2,1)S(1)}, u32[]{:S(2)}, u32[]{:S(2)}) async-start(bf16[16,2,1,4,2880]{4,3,1,2,0:T(4,128)(2,1)} %fusion.116), calls=%async_computation.2 | async-start | bytes 1507328 | tf_op jit(solution)/shard_map/while/body/eval_jaxpr/all_to_all | solution.py:66
  110.2 17.1 %all-to-all-start = ((bf16[16,4,2880]{2,1,0:T(4,128)(2,1)}), bf16[16,4,2880]{2,1,0:T(4,128)(2,1)S(1)}, u32[]{:S(2)}, u32[]{:S(2)}) async-start(bf16[16,4,2880]{2,1,0:T(4,128)(2,1)} %copy.135), calls=%async_computation | async-start | bytes 753664 | tf_op jit(solution)/shard_map/while/body/eval_jaxpr/all_to_all | solution.py:45
  145.8 12.9 %all-to-all-start.3 = ((bf16[2,16,4]{1,2,0:T(4,128)(2,1)}), bf16[2,16,4]{1,2,0:T(4,128)(2,1)S(1)}, u32[]{:S(2)}, u32[]{:S(2)}) async-start(bf16[2,16,4]{1,2,0:T(4,128)(2,1)} %copy.137), calls=%async_computation.3 | async-start | bytes 4096 | tf_op jit(solution)/shard_map/while/body/eval_jaxpr/all_to_all | solution.py:80
  158.6 12.5 %all-to-all-start.1 = ((bf16[2,16,4,2880]{3,2,1,0:T(4,128)(2,1)}), bf16[2,16,4,2880]{3,2,1,0:T(4,128)(2,1)S(1)}, u32[]{:S(2)}, u32[]{:S(2)}) async-start(bf16[2,16,4,2880]{3,2,1,0:T(4,128)(2,1)} %reshape.109), calls=%async_computation.1 | async-start | bytes 1507328 | tf_op jit(solution)/shard_map/while/body/eval_jaxpr/all_to_all | solution.py:77
  171.1 14.1 %all-to-all-start.4 = ((bf16[2,16,4]{2,0,1:T(2,128)(2,1)}), bf16[2,16,4]{2,0,1:T(2,128)(2,1)S(1)}, u32[]{:S(2)}, u32[]{:S(2)}) async-start(bf16[2,16,4]{2,0,1:T(2,128)(2,1)} %copy.138), calls=%async_computation.4 | async-start | bytes 16384 | tf_op jit(solution)/shard_map/while/body/eval_jaxpr/all_to_all | solution.py:79
  185.2 24.2 %all-to-all-start.2 = ((bf16[16,2,1,4,2880]{4,3,1,2,0:T(4,128)(2,1)}), bf16[16,2,1,4,2880]{4,3,1,2,0:T(4,128)(2,1)S(1)}, u32[]{:S(2)}, u32[]{:S(2)}) async-start(bf16[16,2,1,4,2880]{4,3,1,2,0:T(4,128)(2,1)} %fusion.116), calls=%async_computation.2 | async-start | bytes 1507328 | tf_op jit(solution)/shard_map/while/body/eval_jaxpr/all_to_all | solution.py:66
  210.1 0.6 copy-start
